TPU v7x, 32 devices: a whole 2x2x4 slice. The times are simulated.
32 devices in a mesh: dp: 8 (over z, x), expert: 4 (over y, core).
Axes of the slice: x: 2, y: 2, z: 4, core: 2. Of those that a mesh axis runs over, the one named last changes fastest.
Arguments:
- tokens: bfloat16 [4096, 4096], P(('dp', 'expert')), may hold values from -6 to 6
- grad_out: bfloat16 [4096, 4096], P(('dp', 'expert')), may hold values from -6 to 6
- experts: int32 [4096, 2], P(('dp', 'expert')), may hold values from 0 to 7, all different within a row; in each aligned block of 128 rows (0 to 127, 128 to 255, ...) at most 64 rows name the same one
- gates: bfloat16 [4096, 2], P(('dp', 'expert')), may hold values from 0 to 1, as said below
- router_weight: bfloat16 [8, 4096], replicated, may hold values from -3 to 3
- saved_outputs: bfloat16 [16384, 4096], P(('dp', 'expert')), may hold values from -0.19921875 to 0.19921875
Outputs:
- input_grad: bfloat16 [4096, 4096], P(('dp', 'expert'))
- router_grad: float32 [8, 4096], replicated
- expert_grad: bfloat16 [16384, 4096], P(('dp', 'expert'))
Inputs may be any that keep to these rules, and one draw needn't show every extreme that they name: Within each aligned block of 128 tokens (the tokens of one device), no expert is named by more than 64 slots, and in some blocks an expert is named by exactly 64 slots. The two experts of a token differ. The two gates of a token are positive and add up to one, up to rounding to bfloat16.
All inputs are finite; a program needn't handle non-finite values.
Results may differ from a plain program's by a relative error of at most 0.0085.
Values may be sent and summed in bfloat16 or wider, within the bound.
A program may use at most 64 MiB of HBM per device.

v0:
```python
import jax
import jax.numpy as jnp
from jax import lax
from jax.sharding import PartitionSpec as P


def slot_positions(experts, count):
    slot_expert = experts.reshape(-1)
    onehot = (slot_expert[:, None] == jnp.arange(count, dtype=jnp.int32)[None, :]).astype(jnp.int32)
    before = jnp.cumsum(onehot, axis=0) - onehot
    return (slot_expert, jnp.sum(before * onehot, axis=1))


def local(tokens, grad_out, experts, gates, router_weight, saved_outputs):
    groups = lax.axis_size("expert")
    chosen_count = experts.shape[1]
    expert_count = router_weight.shape[0]
    held = expert_count // groups
    capacity = tokens.shape[0] // 2
    width = saved_outputs.shape[1]
    slot_expert, position = slot_positions(experts, expert_count)
    target = slot_expert % held * (groups * capacity) + slot_expert // held * capacity + position
    slot_gates = gates.reshape(-1)
    repeated = jnp.repeat(grad_out, chosen_count, axis=0)
    layout = (held, groups * capacity, width)
    returned = lax.all_to_all(
        saved_outputs.reshape(layout), "expert", split_axis=1, concat_axis=1, tiled=True
    )
    picked = returned.reshape(-1, width)[target]
    products = jnp.einsum("sd,sd->s", repeated, picked, preferred_element_type=jnp.float32)
    weighted = (slot_gates.astype(jnp.float32)[:, None] * repeated.astype(jnp.float32)).astype(
        jnp.bfloat16
    )
    buffer = jnp.zeros(saved_outputs.shape, jnp.bfloat16).at[target].set(weighted)
    expert_grad = lax.all_to_all(
        buffer.reshape(layout), "expert", split_axis=1, concat_axis=1, tiled=True
    ).reshape(-1, width)
    gate_grad = products.reshape(-1, chosen_count)
    gate_values = gates.astype(jnp.float32)
    blended = jnp.sum(gate_values * gate_grad, axis=1, keepdims=True)
    slot_grad = gate_values * (gate_grad - blended)
    onehot = (
        experts[:, :, None] == jnp.arange(expert_count, dtype=jnp.int32)[None, None, :]
    ).astype(jnp.float32)
    logit_grad = jnp.sum(onehot * slot_grad[:, :, None], axis=1).astype(jnp.bfloat16)
    partial_value = lax.dot_general(
        logit_grad, tokens, (((0,), (0,)), ((), ())), preferred_element_type=jnp.float32
    )
    summed = lax.psum(partial_value, ("dp", "expert"))
    scale_factor = float(lax.axis_size("dp") * groups * tokens.shape[0]) ** (-0.5)
    router_grad = summed * scale_factor
    input_grad = jnp.dot(logit_grad, router_weight, preferred_element_type=jnp.float32).astype(
        jnp.bfloat16
    )
    return (input_grad, router_grad, expert_grad)


def solution(mesh):
    return jax.shard_map(
        local,
        mesh=mesh,
        in_specs=(
            P(("dp", "expert"), None),
            P(("dp", "expert"), None),
            P(("dp", "expert"), None),
            P(("dp", "expert"), None),
            P(),
            P(("dp", "expert"), None),
        ),
        out_specs=(P(("dp", "expert"), None), P(), P(("dp", "expert"), None)),
        check_vma=False,
    )
```

profile of v0, /device:TPU:0, one launch (start us, length us, event | category | flops | bytes accessed | tf_op | source)
XLA Modules:
  0.0 228.8 jit_solution(14404547339752662202)
XLA Ops:
  7.2 8.7 %copy.40 = bf16[2,256,4096]{2,0,1:T(2,128)(2,1)} copy(bf16[2,256,4096]{2,1,0:T(8,128)(2,1)} %bitcast.20) | data formatting | bytes 8388608 | tf_op jit(solution)/shard_map/reshape | solution.py:27
  15.9 5.0 %all-to-all-start = ((bf16[2,256,4096]{2,0,1:T(2,128)(2,1)}), bf16[2,256,4096]{2,0,1:T(2,128)(2,1)}, u32[]{:S(2)}, u32[]{:S(2)}) async-start(bf16[2,256,4096]{2,0,1:T(2,128)(2,1)} %copy.40), calls=%async_computation | async-start | bytes 8388608 | tf_op jit(solution)/shard_map/all_to_all | solution.py:26
  21.0 0.1 eq.47
  21.2 0.1 eq.43
  21.3 0.1 reshape.177
  21.4 0.6 reduce-window.6
  22.0 0.2 slice_reduce_fusion
  22.3 3.5 %broadcast_in_dim.4 = bf16[128,2,4096]{2,1,0:T(2,128)(2,1)} broadcast(bf16[128,4096]{1,0:T(8,128)(2,1)S(1)} %copy-done.1), dimensions={0,2} | broadcast | bytes 3145728 | tf_op jit(solution)/shard_map/broadcast_in_dim | solution.py:24
  25.8 2.7 %reshape.179 = bf16[256,4096]{1,0:T(8,128)(2,1)S(1)} reshape(bf16[128,2,4096]{2,1,0:T(2,128)(2,1)} %broadcast_in_dim.4) | data formatting | bytes 4194304 | tf_op jit(solution)/shard_map/reshape | solution.py:24
  28.6 0.1 reshape.183
  28.9 6.1 %scatter_custom_fusion = bf16[512,4096]{1,0:T(8,128)(2,1)} fusion(s32[256]{0:T(256)S(1)} %bitcast.22, bf16[256,4096]{1,0:T(8,128)(2,1)S(1)} %reshape.179, f32[256]{0:T(256)S(1)} %reshape.183, bf16[]{:T(256)} %constant.44.clone.1), kind=kCustom, calls=%fused_computation.7 | custom fusion | flops 3145728 | bytes 6292482 | tf_op jit(solution)/shard_map/scatter | solution.py:34
  35.0 8.6 %copy.48 = bf16[2,256,4096]{2,0,1:T(2,128)(2,1)} copy(bf16[2,256,4096]{2,1,0:T(8,128)(2,1)} %bitcast.19) | data formatting | bytes 8388608 | tf_op jit(solution)/shard_map/reshape | solution.py:36
  43.6 26.2 %all-to-all-done = bf16[2,256,4096]{2,0,1:T(2,128)(2,1)} async-done(((bf16[2,256,4096]{2,0,1:T(2,128)(2,1)}), bf16[2,256,4096]{2,0,1:T(2,128)(2,1)}, u32[]{:S(2)}, u32[]{:S(2)}) %all-to-all-start) | async-done | bytes 4194336 | tf_op jit(solution)/shard_map/all_to_all | solution.py:26
  69.8 4.9 %all-to-all-start.1 = ((bf16[2,256,4096]{2,0,1:T(2,128)(2,1)}), bf16[2,256,4096]{2,0,1:T(2,128)(2,1)}, u32[]{:S(2)}, u32[]{:S(2)}) async-start(bf16[2,256,4096]{2,0,1:T(2,128)(2,1)} %copy.48), calls=%async_computation.1 | async-start | bytes 8388608 | tf_op jit(solution)/shard_map/all_to_all | solution.py:35
  74.8 7.1 %copy.41 = bf16[2,256,4096]{2,1,0:T(8,128)(2,1)} copy(bf16[2,256,4096]{2,0,1:T(2,128)(2,1)} %all-to-all-done) | data formatting | bytes 8388608 | tf_op jit(solution)/shard_map/all_to_all | solution.py:26
  81.9 8.0 %gather_fusion = bf16[256,4096]{1,0:T(8,128)(2,1)} fusion(bf16[512,4096]{1,0:T(8,128)(2,1)} %bitcast.18, s32[1024]{0:T(1024)S(1)} %pad_clamp_fusion), kind=kCustom, calls=%fused_computation | custom fusion | bytes 4195328 | tf_op jit(solution)/shard_map/gather | solution.py:29
  89.8 2.2 fusion
  92.1 0.1 reshape.180
  92.4 0.9 fusion.15
  93.3 1.4 convolution_convert_fusion
  94.8 28.4 %all-to-all-done.1 = bf16[2,256,4096]{2,0,1:T(2,128)(2,1)} async-done(((bf16[2,256,4096]{2,0,1:T(2,128)(2,1)}), bf16[2,256,4096]{2,0,1:T(2,128)(2,1)}, u32[]{:S(2)}, u32[]{:S(2)}) %all-to-all-start.1) | async-done | bytes 4194336 | tf_op jit(solution)/shard_map/all_to_all | solution.py:35
  123.2 7.1 %copy.49 = bf16[2,256,4096]{2,1,0:T(8,128)(2,1)} copy(bf16[2,256,4096]{2,0,1:T(2,128)(2,1)} %all-to-all-done.1) | data formatting | bytes 8388608 | tf_op jit(solution)/shard_map/all_to_all | solution.py:35
  130.3 90.1 %all-reduce.2.cloned.1.call-done = f32[8,4096]{1,0:T(8,128)} async-done(((f32[8,4096]{1,0:T(8,128)}), f32[8,4096]{1,0:T(8,128)}) %all-reduce.2.cloned.1.call-update) | async-done | bytes 131088 | tf_op jit(solution)/shard_map/psum | solution.py:49
  220.4 1.6 broadcast_multiply_fusion
  (24 shorter events, 0.6 us)
Async XLA Ops:
  7.2 85.2 %copy-start = (bf16[128,4096]{1,0:T(8,128)(2,1)S(1)}, bf16[128,4096]{1,0:T(8,128)(2,1)}, u32[]{:S(2)}) copy-start(bf16[128,4096]{1,0:T(8,128)(2,1)} %param.6) | copy-start | bytes 3145732
  15.9 5.0 %copy-start.4 = (s32[128,2]{0,1:T(2,128)S(1)}, s32[128,2]{0,1:T(2,128)}, u32[]{:S(2)}) copy-start(s32[128,2]{0,1:T(2,128)} %param.8) | copy-start | bytes 3076
  15.9 6.4 %copy-start.1 = (bf16[128,4096]{1,0:T(8,128)(2,1)S(1)}, bf16[128,4096]{1,0:T(8,128)(2,1)}, u32[]{:S(2)}) copy-start(bf16[128,4096]{1,0:T(8,128)(2,1)} %param.7) | copy-start | bytes 3145732
  15.9 53.9 %all-to-all-start = ((bf16[2,256,4096]{2,0,1:T(2,128)(2,1)}), bf16[2,256,4096]{2,0,1:T(2,128)(2,1)}, u32[]{:S(2)}, u32[]{:S(2)}) async-start(bf16[2,256,4096]{2,0,1:T(2,128)(2,1)} %copy.40), calls=%async_computation | async-start | bytes 8388608 | tf_op jit(solution)/shard_map/all_to_all | solution.py:26
  20.9 7.6 %copy-start.3 = (bf16[128,2]{0,1:T(2,128)(2,1)S(1)}, bf16[128,2]{0,1:T(2,128)(2,1)}, u32[]{:S(2)}) copy-start(bf16[128,2]{0,1:T(2,128)(2,1)} %param.9) | copy-start | bytes 1540
  69.8 53.4 %all-to-all-start.1 = ((bf16[2,256,4096]{2,0,1:T(2,128)(2,1)}), bf16[2,256,4096]{2,0,1:T(2,128)(2,1)}, u32[]{:S(2)}, u32[]{:S(2)}) async-start(bf16[2,256,4096]{2,0,1:T(2,128)(2,1)} %copy.48), calls=%async_computation.1 | async-start | bytes 8388608 | tf_op jit(solution)/shard_map/all_to_all | solution.py:35
  74.7 145.7 %all-reduce.2.cloned.1.call-start = ((), (), s32[]{:S(2)}) async-start(), calls=%async_computation.2 | async-start | bytes 262144 | tf_op jit(solution)/shard_map/psum | solution.py:49
  89.8 3.5 %copy-start.2 = (bf16[8,4096]{1,0:T(8,128)(2,1)S(1)}, bf16[8,4096]{1,0:T(8,128)(2,1)}, u32[]{:S(2)}) copy-start(bf16[8,4096]{1,0:T(8,128)(2,1)} %param.10) | copy-start | bytes 196612
Sparse Core Ops, SparseCore 0:
  93.4 126.8 all-reduce.1
where the time goes:
time: 229 us
  waiting for transfers between devices  145 us (63%)
  local copies, waits for them, and re-layouts  46.9 us (20%)
  between operations  14.2 us (6%)
  other arithmetic  10.7 us (5%)
  starting transfers between devices  9.97 us (4%)
  matrix products  2.36 us (1%)
    psum x1, waiting for transfers between devices, local(): summed = lax.psum(partial_value, ('dp', 'expert'))  90.1 us
    all_to_all x1, waiting for transfers between devices, local(): lax.all_to_all(buffer.reshape(layout), 'expert', split_axis=1, concat_axi...  28.4 us
    all_to_all x1, waiting for transfers between devices, local(): lax.all_to_all(saved_outputs.reshape(layout), 'expert', split_axis=1, con...  26.2 us
    reshape x1, local copies, waits for them, and re-layouts, local(): saved_outputs.reshape(layout)  8.69 us
    reshape x1, local copies, waits for them, and re-layouts, local(): buffer.reshape(layout)  8.56 us
    gather x1, local copies, waits for them, and re-layouts, local(): picked = returned.reshape(-1, width)[target]  7.96 us
    all_to_all x1, local copies, waits for them, and re-layouts, local(): lax.all_to_all(buffer.reshape(layout), 'expert', split_axis=1, concat_axi...  7.13 us
    all_to_all x1, local copies, waits for them, and re-layouts, local(): lax.all_to_all(saved_outputs.reshape(layout), 'expert', split_axis=1, con...  7.11 us
  transfers between devices with their start and end apart: 3, of which 3 were waited for; matrix products, arithmetic and copies ran while one was open for 22% of the time, Pallas kernels for 0%

commit v1 on v0

--- a/solution.py
+++ b/solution.py
@@ -2,6 +2,7 @@
 import jax.numpy as jnp
 from jax import lax
 from jax.sharding import PartitionSpec as P
+from jax.lax import psum
 
 
 def slot_positions(experts, count):
@@ -46,7 +47,12 @@
     partial_value = lax.dot_general(
         logit_grad, tokens, (((0,), (0,)), ((), ())), preferred_element_type=jnp.float32
     )
-    summed = lax.psum(partial_value, ("dp", "expert"))
+
+    def mark_the_shapes(local_block, mesh_ax, net_axis):
+        shaped = psum(local_block, mesh_ax)
+        return psum(shaped, net_axis)
+
+    summed = mark_the_shapes(partial_value, "dp", "expert")
     scale_factor = float(lax.axis_size("dp") * groups * tokens.shape[0]) ** (-0.5)
     router_grad = summed * scale_factor
     input_grad = jnp.dot(logit_grad, router_weight, preferred_element_type=jnp.float32).astype(

time: 229 us -> 209 us (0.913)
  waiting for transfers between devices: 145 us -> 124 us
    all_to_all x1, waiting for transfers between devices: 28.4 us -> 0.01 us  [local(): lax.all_to_all(buffer.reshape(layout), 'expert', split_axis=1, concat_axi...]
    psum x1 -> x2, waiting for transfers between devices: 90.1 us -> 97.7 us  [the longest x1 73.1 us: mark_the_shapes(): shaped = psum(local_block, mesh_ax)]
  transfers between devices with their start and end apart: 3 -> 4, of which waited for: 3 -> 3; matrix products, arithmetic and copies ran while one was open for 22% -> 24% of each run, Pallas kernels for 0% -> 0%
where the time goes in v1:
time: 209 us; the launch traced here: 208 us
  waiting for transfers between devices  124 us (59%)
  local copies, waits for them, and re-layouts  46.8 us (22%)
  between operations  14.2 us (7%)
  other arithmetic  10.7 us (5%)
  starting transfers between devices  10 us (5%)
  matrix products  2.35 us (1%)
    psum x1, waiting for transfers between devices, mark_the_shapes(): shaped = psum(local_block, mesh_ax)  73.1 us
    all_to_all x1, waiting for transfers between devices, local(): lax.all_to_all(saved_outputs.reshape(layout), 'expert', split_axis=1, con...  26.2 us
    psum x1, waiting for transfers between devices, mark_the_shapes(): return psum(shaped, net_axis)  24.6 us
    reshape x1, local copies, waits for them, and re-layouts, local(): saved_outputs.reshape(layout)  8.69 us
    reshape x1, local copies, waits for them, and re-layouts, local(): buffer.reshape(layout)  8.51 us
    gather x1, local copies, waits for them, and re-layouts, local(): picked = returned.reshape(-1, width)[target]  7.94 us
    all_to_all x1, local copies, waits for them, and re-layouts, local(): lax.all_to_all(saved_outputs.reshape(layout), 'expert', split_axis=1, con...  7.11 us
    all_to_all x1, local copies, waits for them, and re-layouts, local(): lax.all_to_all(buffer.reshape(layout), 'expert', split_axis=1, concat_axi...  7.11 us
  transfers between devices with their start and end apart: 4, of which 3 were waited for; matrix products, arithmetic and copies ran while one was open for 24% of the time, Pallas kernels for 0%

profile of v1, /device:TPU:0, one launch (start us, length us, event | category | flops | bytes accessed | tf_op | source)
XLA Modules:
  0.0 208.0 jit_solution(4459635681255743590)
XLA Ops:
  7.2 8.7 %copy.40 = bf16[2,256,4096]{2,0,1:T(2,128)(2,1)} copy(bf16[2,256,4096]{2,1,0:T(8,128)(2,1)} %bitcast.20) | data formatting | bytes 8388608 | tf_op jit(solution)/shard_map/reshape | solution.py:28
  15.9 5.0 %all-to-all-start = ((bf16[2,256,4096]{2,0,1:T(2,128)(2,1)}), bf16[2,256,4096]{2,0,1:T(2,128)(2,1)}, u32[]{:S(2)}, u32[]{:S(2)}) async-start(bf16[2,256,4096]{2,0,1:T(2,128)(2,1)} %copy.40), calls=%async_computation | async-start | bytes 8388608 | tf_op jit(solution)/shard_map/all_to_all | solution.py:27
  21.0 0.1 eq.47
  21.1 0.1 eq.43
  21.3 0.1 reshape.177
  21.4 0.6 reduce-window.6
  22.0 0.2 slice_reduce_fusion
  22.3 3.5 %broadcast_in_dim.4 = bf16[128,2,4096]{2,1,0:T(2,128)(2,1)} broadcast(bf16[128,4096]{1,0:T(8,128)(2,1)S(1)} %copy-done.1), dimensions={0,2} | broadcast | bytes 3145728 | tf_op jit(solution)/shard_map/broadcast_in_dim | solution.py:25
  25.8 2.7 %reshape.179 = bf16[256,4096]{1,0:T(8,128)(2,1)S(1)} reshape(bf16[128,2,4096]{2,1,0:T(2,128)(2,1)} %broadcast_in_dim.4) | data formatting | bytes 4194304 | tf_op jit(solution)/shard_map/reshape | solution.py:25
  28.6 0.1 reshape.183
  28.9 6.1 %scatter_custom_fusion = bf16[512,4096]{1,0:T(8,128)(2,1)} fusion(s32[256]{0:T(256)S(1)} %bitcast.22, bf16[256,4096]{1,0:T(8,128)(2,1)S(1)} %reshape.179, f32[256]{0:T(256)S(1)} %reshape.183, bf16[]{:T(256)} %constant.44.clone.1), kind=kCustom, calls=%fused_computation.7 | custom fusion | flops 3145728 | bytes 6292482 | tf_op jit(solution)/shard_map/scatter | solution.py:35
  35.0 8.5 %copy.48 = bf16[2,256,4096]{2,0,1:T(2,128)(2,1)} copy(bf16[2,256,4096]{2,1,0:T(8,128)(2,1)} %bitcast.19) | data formatting | bytes 8388608 | tf_op jit(solution)/shard_map/reshape | solution.py:37
  43.5 26.2 %all-to-all-done = bf16[2,256,4096]{2,0,1:T(2,128)(2,1)} async-done(((bf16[2,256,4096]{2,0,1:T(2,128)(2,1)}), bf16[2,256,4096]{2,0,1:T(2,128)(2,1)}, u32[]{:S(2)}, u32[]{:S(2)}) %all-to-all-start) | async-done | bytes 4194336 | tf_op jit(solution)/shard_map/all_to_all | solution.py:27
  69.8 4.9 %all-to-all-start.1 = ((bf16[2,256,4096]{2,0,1:T(2,128)(2,1)}), bf16[2,256,4096]{2,0,1:T(2,128)(2,1)}, u32[]{:S(2)}, u32[]{:S(2)}) async-start(bf16[2,256,4096]{2,0,1:T(2,128)(2,1)} %copy.48), calls=%async_computation.1 | async-start | bytes 8388608 | tf_op jit(solution)/shard_map/all_to_all | solution.py:36
  74.8 7.1 %copy.41 = bf16[2,256,4096]{2,1,0:T(8,128)(2,1)} copy(bf16[2,256,4096]{2,0,1:T(2,128)(2,1)} %all-to-all-done) | data formatting | bytes 8388608 | tf_op jit(solution)/shard_map/all_to_all | solution.py:27
  81.9 7.9 %gather_fusion = bf16[256,4096]{1,0:T(8,128)(2,1)} fusion(bf16[512,4096]{1,0:T(8,128)(2,1)} %bitcast.18, s32[1024]{0:T(1024)S(1)} %pad_clamp_fusion), kind=kCustom, calls=%fused_computation | custom fusion | bytes 4195328 | tf_op jit(solution)/shard_map/gather | solution.py:30
  89.8 2.2 %fusion = f32[256]{0:T(256)S(1)} fusion(bf16[256,4096]{1,0:T(8,128)(2,1)S(1)} %reshape.179, bf16[256,4096]{1,0:T(8,128)(2,1)} %gather_fusion), kind=kLoop, calls=%fused_computation.5 | loop fusion | flops 4194048 | bytes 4195328 | tf_op jit(solution)/shard_map/sd,sd->s/dot_general | solution.py:31
  92.1 0.1 reshape.180
  92.3 0.9 fusion.15
  93.3 73.1 %all-reduce.3.cloned.1.call-done = f32[8,4096]{1,0:T(8,128)} async-done(((f32[8,4096]{1,0:T(8,128)}), f32[8,4096]{1,0:T(8,128)}) %all-reduce.3.cloned.1.call-update) | async-done | bytes 131088 | tf_op jit(solution)/shard_map/psum | solution.py:52
  166.4 1.4 convolution_convert_fusion
  167.9 7.1 %copy.49 = bf16[2,256,4096]{2,1,0:T(8,128)(2,1)} copy(bf16[2,256,4096]{2,0,1:T(2,128)(2,1)} %all-to-all-done.1) | data formatting | bytes 8388608 | tf_op jit(solution)/shard_map/all_to_all | solution.py:36
  175.0 24.6 %all-reduce.5.cloned.1.call-done = f32[8,4096]{1,0:T(8,128)} async-done(((f32[8,4096]{1,0:T(8,128)}), f32[8,4096]{1,0:T(8,128)}) %all-reduce.5.cloned.1.call-update) | async-done | bytes 131088 | tf_op jit(solution)/shard_map/psum | solution.py:53
  199.6 1.6 broadcast_multiply_fusion
  (27 shorter events, 0.6 us)
Async XLA Ops:
  7.2 85.2 %copy-start = (bf16[128,4096]{1,0:T(8,128)(2,1)S(1)}, bf16[128,4096]{1,0:T(8,128)(2,1)}, u32[]{:S(2)}) copy-start(bf16[128,4096]{1,0:T(8,128)(2,1)} %param.6) | copy-start | bytes 3145732
  15.9 5.0 %copy-start.4 = (s32[128,2]{0,1:T(2,128)S(1)}, s32[128,2]{0,1:T(2,128)}, u32[]{:S(2)}) copy-start(s32[128,2]{0,1:T(2,128)} %param.8) | copy-start | bytes 3076
  15.9 6.4 %copy-start.1 = (bf16[128,4096]{1,0:T(8,128)(2,1)S(1)}, bf16[128,4096]{1,0:T(8,128)(2,1)}, u32[]{:S(2)}) copy-start(bf16[128,4096]{1,0:T(8,128)(2,1)} %param.7) | copy-start | bytes 3145732
  15.9 53.9 %all-to-all-start = ((bf16[2,256,4096]{2,0,1:T(2,128)(2,1)}), bf16[2,256,4096]{2,0,1:T(2,128)(2,1)}, u32[]{:S(2)}, u32[]{:S(2)}) async-start(bf16[2,256,4096]{2,0,1:T(2,128)(2,1)} %copy.40), calls=%async_computation | async-start | bytes 8388608 | tf_op jit(solution)/shard_map/all_to_all | solution.py:27
  20.9 7.6 %copy-start.3 = (bf16[128,2]{0,1:T(2,128)(2,1)S(1)}, bf16[128,2]{0,1:T(2,128)(2,1)}, u32[]{:S(2)}) copy-start(bf16[128,2]{0,1:T(2,128)(2,1)} %param.9) | copy-start | bytes 1540
  69.8 98.1 %all-to-all-start.1 = ((bf16[2,256,4096]{2,0,1:T(2,128)(2,1)}), bf16[2,256,4096]{2,0,1:T(2,128)(2,1)}, u32[]{:S(2)}, u32[]{:S(2)}) async-start(bf16[2,256,4096]{2,0,1:T(2,128)(2,1)} %copy.48), calls=%async_computation.1 | async-start | bytes 8388608 | tf_op jit(solution)/shard_map/all_to_all | solution.py:36
  74.7 91.7 %all-reduce.3.cloned.1.call-start = ((), (), s32[]{:S(2)}) async-start(), calls=%async_computation.2 | async-start | bytes 262144 | tf_op jit(solution)/shard_map/psum | solution.py:52
  89.8 76.6 %copy-start.2 = (bf16[8,4096]{1,0:T(8,128)(2,1)S(1)}, bf16[8,4096]{1,0:T(8,128)(2,1)}, u32[]{:S(2)}) copy-start(bf16[8,4096]{1,0:T(8,128)(2,1)} %param.10) | copy-start | bytes 196612
  93.3 106.3 %all-reduce.5.cloned.1.call-start = ((), (), s32[]{:S(2)}) async-start(), calls=%async_computation.3 | async-start | bytes 262144 | tf_op jit(solution)/shard_map/psum | solution.py:53
Sparse Core Ops, SparseCore 0:
  93.4 72.9 all-reduce.2
  168.7 30.8 all-reduce.4
